TPU v7x, 128 devices: a whole 4x4x4 slice. The times are simulated.
128 devices in a mesh: dp: 8 (over x, core), pipe: 4 (over y), tensor: 4 (over z).
Axes of the slice: x: 4, y: 4, z: 4, core: 2. Of those that a mesh axis runs over, the one named last changes fastest.
Arguments:
- support_tokens: int32 [64, 32], P(('dp', 'pipe')), may hold values from 0 to 64127
- support_lengths: int32 [64], P(('dp', 'pipe')), may hold values from 1 to 32
- support_labels: int32 [64, 1], P(('dp', 'pipe')), may hold values from 0 to 31
- query_tokens: int32 [32, 32], P(('dp', 'pipe')), may hold values from 0 to 64127
- query_lengths: int32 [32], P(('dp', 'pipe')), may hold values from 1 to 32
- query_episodes: int32 [32], P(('dp', 'pipe')), may hold values from 0 to 1
- embedding: bfloat16 [64128, 4096], P(('dp', 'pipe'), 'tensor'), may hold values from -18 to 18
- attn_gain: float32 [4, 4096], P('pipe'), may hold values from 0.5 to 1.5
- query_weight: bfloat16 [4, 4096, 4096], P('pipe', None, 'tensor'), may hold values from -1 to 1
- key_weight: bfloat16 [4, 4096, 1024], P('pipe', None, 'tensor'), may hold values from -16 to 16
- value_weight: bfloat16 [4, 4096, 1024], P('pipe', None, 'tensor'), may hold values from -0.09375 to 0.09375
- out_weight: bfloat16 [4, 4096, 4096], P('pipe', 'tensor'), may hold values from -0.09375 to 0.09375
- final_gain: float32 [4096], replicated, may hold values from 0.5 to 1.5
Outputs:
- prototypes: float32 [32, 4096], P(None, 'tensor')
- logits: float32 [32, 16], P(('dp', 'pipe'))
Inputs may be any that keep to these rules, and one draw needn't show every extreme that they name: `support_labels`: every class is the label of at least one support sequence.
All inputs are finite; a program needn't handle non-finite values.
Results may differ from a plain program's by a relative error of at most 0.024.
Values may be sent and summed in bfloat16 or wider, within the bound.
A program may use at most 128 MiB of HBM per device.

v0:
```python
import math
import jax
import jax.numpy as jnp
from jax import lax
from jax.sharding import PartitionSpec as P

D = 4096
HEAD_DIM = 128
WAYS = 16
EPISODES = 2
epsilon = 1e-05
rotary_base = 500000.0


def in_order(blocks, dim):
    blocks = jnp.moveaxis(blocks, 0, dim)
    dims = blocks.shape
    return blocks.reshape(*dims[:dim], dims[dim] * dims[dim + 1], *dims[dim + 2 :])


def sent_to_all(shard, axis):
    copies = jnp.broadcast_to(shard, (lax.axis_size(axis), *shard.shape))
    return lax.all_to_all(copies, axis, split_axis=0, concat_axis=0, tiled=True)


def collect(shard, axis, dim):
    return in_order(sent_to_all(shard, axis), dim)


def split_up(shard, dim, length):
    dims = shard.shape
    blocks = shard.reshape(*dims[:dim], length, dims[dim] // length, *dims[dim + 1 :])
    return jnp.moveaxis(blocks, dim, 0)


def sum_at_owner(shard, axis, dim):
    length = lax.axis_size(axis)
    blocks = lax.all_to_all(split_up(shard, dim, length), axis, 0, 0, tiled=True)
    return jnp.sum(blocks.astype(jnp.float32), axis=0)


def passed_along(block, axis, distance):
    devices = range(lax.axis_size(axis))
    route = [((i - distance) % len(devices), i) for i in devices]
    return lax.ppermute(block, axis, route)


def over_copies(shard, axis):
    return sent_to_all(shard, axis).astype(jnp.float32).sum(axis=0)


def rotate(heads_in, seq_len):
    half_dim = HEAD_DIM // 2
    freqs = jnp.exp(
        -math.log(rotary_base) * jnp.arange(half_dim, dtype=jnp.float32) * (2.0 / HEAD_DIM)
    )
    angles = jnp.arange(seq_len, dtype=jnp.float32)[:, None] * freqs[None, :]
    cosine = jnp.cos(angles)[None, :, None, :]
    sine = jnp.sin(angles)[None, :, None, :]
    first_half = heads_in[..., :half_dim]
    second_half = heads_in[..., half_dim:]
    return jnp.concatenate(
        [first_half * cosine - second_half * sine, second_half * cosine + first_half * sine],
        axis=-1,
    )


def whole_rows(hidden):
    return collect(hidden, "tensor", 1)


def whole_values(full_rows, gain_vector):
    values = full_rows.astype(jnp.float32)
    mean_square = jnp.mean(values * values, axis=-1, keepdims=True)
    return values * lax.rsqrt(mean_square + epsilon) * gain_vector


def shards(
    support_tokens,
    support_lengths,
    support_labels,
    query_tokens,
    query_lengths,
    query_episodes,
    embedding,
    attn_gain,
    query_weight,
    key_weight,
    value_weight,
    out_weight,
    final_gain,
):
    group_count = lax.axis_size(("dp", "pipe"))
    sections = lax.axis_size("pipe")
    sup_dev, seq_len = support_tokens.shape
    qry_dev = query_tokens.shape[0]
    seq_count = sup_dev + qry_dev
    row_count = seq_count * seq_len
    table_rows, width = embedding.shape
    column_start = lax.axis_index("tensor") * width
    all_support, all_query, every_sup_len, every_qry_len = (
        lax.all_gather(support_tokens, ("dp", "pipe"), axis=0, tiled=True),
        lax.all_gather(query_tokens, ("dp", "pipe"), axis=0, tiled=True),
        lax.all_gather(support_lengths, ("dp", "pipe"), axis=0, tiled=True),
        lax.all_gather(query_lengths, ("dp", "pipe"), axis=0, tiled=True),
    )
    token_flat = jnp.concatenate(
        [all_support.reshape(group_count, sup_dev * seq_len), all_query], axis=1
    ).reshape(group_count * row_count)
    local_ids = token_flat - lax.axis_index(("dp", "pipe")) * table_rows
    inside = (local_ids >= 0) & (local_ids < table_rows)
    picked = jnp.take(embedding, jnp.clip(local_ids, 0, table_rows - 1), axis=0)
    picked = jnp.where(inside[:, None], picked, jnp.zeros_like(picked))
    replies = lax.all_to_all(picked, ("dp", "pipe"), split_axis=0, concat_axis=0, tiled=True)
    hidden = jnp.sum(
        replies.reshape(group_count, row_count, width).astype(jnp.float32), axis=0
    ).astype(jnp.bfloat16)
    seq_lengths = jnp.concatenate([support_lengths, query_lengths], axis=0)
    query_proj = query_weight[0]
    key_proj = key_weight[0]
    value_proj = value_weight[0]
    out_proj = out_weight[0]
    gain_vector = attn_gain[0]
    local_heads = query_proj.shape[1] // HEAD_DIM
    local_groups = key_proj.shape[1] // HEAD_DIM
    group_size = local_heads // local_groups
    w_in = jnp.concatenate([query_proj, key_proj, value_proj], axis=1)
    query_cols = local_heads * HEAD_DIM
    key_cols = local_groups * HEAD_DIM
    positions = jnp.arange(seq_len)
    causal = positions[None, :] <= positions[:, None]

    def section_block(stream, lengths_here):
        normed = whole_values(whole_rows(stream), gain_vector).astype(jnp.bfloat16)
        projected = jnp.dot(normed, w_in, preferred_element_type=jnp.float32)
        query_heads = projected[:, :query_cols].reshape(seq_count, seq_len, local_heads, HEAD_DIM)
        key_heads = projected[:, query_cols : query_cols + key_cols].reshape(
            seq_count, seq_len, local_groups, HEAD_DIM
        )
        value_heads = (
            projected[:, query_cols + key_cols :]
            .reshape(seq_count, seq_len, local_groups, HEAD_DIM)
            .astype(jnp.bfloat16)
        )
        query_heads = (
            rotate(query_heads, seq_len)
            .astype(jnp.bfloat16)
            .reshape(seq_count, seq_len, local_groups, group_size, HEAD_DIM)
        )
        key_heads = rotate(key_heads, seq_len).astype(jnp.bfloat16)
        scores = jnp.einsum(
            "sikgd,sjkd->skgij", query_heads, key_heads, preferred_element_type=jnp.float32
        ) / math.sqrt(HEAD_DIM)
        visible = causal[None, :, :] & (positions[None, None, :] < lengths_here[:, None, None])
        scores = jnp.where(visible[:, None, None, :, :], scores, -1e30)
        weights = jax.nn.softmax(scores, axis=-1).astype(jnp.bfloat16)
        mixed = jnp.einsum(
            "skgij,sjkd->sikgd", weights, value_heads, preferred_element_type=jnp.float32
        )
        mixed = mixed.astype(jnp.bfloat16).reshape(row_count, query_cols)
        partial_out = jnp.dot(mixed, out_proj, preferred_element_type=jnp.float32)
        summed = sum_at_owner(partial_out.astype(jnp.bfloat16), "tensor", 1)
        return (stream.astype(jnp.float32) + summed).astype(jnp.bfloat16)

    section_index = lax.axis_index("pipe")
    dp_base = lax.axis_index("dp") * sections

    def tick(tick_index, stream):
        held_group = dp_base + (section_index - tick_index) % sections
        sup_part = lax.dynamic_slice_in_dim(every_sup_len, held_group * sup_dev, sup_dev)
        qry_part = lax.dynamic_slice_in_dim(every_qry_len, held_group * qry_dev, qry_dev)
        lengths_here = jnp.concatenate([sup_part, qry_part], axis=0)
        first_tick = (tick_index - section_index) % sections
        active = (first_tick <= tick_index) & (tick_index < first_tick + sections)
        computed = section_block(stream, lengths_here)
        stream = jnp.where(active, computed, stream)
        return passed_along(stream, "pipe", 1)

    hidden = lax.fori_loop(0, 2 * sections, tick, hidden)
    final = lax.dynamic_slice_in_dim(
        whole_values(whole_rows(hidden), final_gain), column_start, width, 1
    )
    live = (positions[None, :] < seq_lengths[:, None]).astype(jnp.float32)
    pooled = jnp.sum(
        final.reshape(seq_count, seq_len, width) * live[:, :, None], axis=1
    ) / seq_lengths[:, None].astype(jnp.float32)
    support_pooled = pooled[:sup_dev]
    query_pooled = pooled[sup_dev:]
    class_count_all = EPISODES * WAYS
    onehot = (support_labels[:, 0][:, None] == jnp.arange(class_count_all)[None, :]).astype(
        jnp.float32
    )
    class_total = jnp.dot(onehot.T, support_pooled, precision=lax.Precision.HIGHEST)
    class_count = jnp.sum(onehot, axis=0)
    class_total, class_count = (
        over_copies(class_total.astype(jnp.bfloat16), ("dp", "pipe")).astype(jnp.float32),
        over_copies(class_count.astype(jnp.bfloat16), ("dp", "pipe")).astype(jnp.float32),
    )
    prototypes = class_total / class_count[:, None]
    episode_pick = (query_episodes[:, None] == jnp.arange(EPISODES)[None, :]).astype(jnp.float32)
    chosen = jnp.einsum(
        "qe,ewc->qwc",
        episode_pick,
        prototypes.reshape(EPISODES, WAYS, width),
        precision=lax.Precision.HIGHEST,
    )
    partial_distance = jnp.sum((query_pooled[:, None, :] - chosen) ** 2, axis=-1)
    distance = lax.psum(partial_distance, "tensor")
    logits = -distance / math.sqrt(D)
    return (prototypes, logits)


def solution(mesh):
    return jax.shard_map(
        shards,
        mesh=mesh,
        in_specs=(
            P(("dp", "pipe"), None),
            P(("dp", "pipe")),
            P(("dp", "pipe"), None),
            P(("dp", "pipe"), None),
            P(("dp", "pipe")),
            P(("dp", "pipe")),
            P(("dp", "pipe"), "tensor"),
            P("pipe", None),
            P("pipe", None, "tensor"),
            P("pipe", None, "tensor"),
            P("pipe", None, "tensor"),
            P("pipe", "tensor", None),
            P(),
        ),
        out_specs=(P(None, "tensor"), P(("dp", "pipe"), None)),
        check_vma=False,
    )
```

profile of v0, /device:TPU:0, one launch (start us, length us, event | category | flops | bytes accessed | tf_op | source)
XLA Modules:
  0.0 681.9 jit_solution(12424556584828293104)
XLA Ops:
  0.6 33.8 %all-gather.1 = s32[32,1,32]{2,1,0:T(1,128)S(1)} all-gather(s32[1,1,32]{2,1,0:T(1,128)} %bitcast.148), channel_id=1, replica_groups=mesh['dp'=8,'pipe'=4,'tensor'=4] {'dp','pipe'}, dimensions={0}, use_global_device_ids=true | all-gather | bytes 4224 | tf_op jit(solution)/shard_map/all_gather | solution.py:103
  34.4 36.5 %all-gather = s32[32,2,32]{2,1,0:T(2,128)S(1)} all-gather(s32[1,2,32]{2,1,0:T(2,128)} %bitcast.144), channel_id=1, replica_groups=mesh['dp'=8,'pipe'=4,'tensor'=4] {'dp','pipe'}, dimensions={0}, use_global_device_ids=true | all-gather | bytes 8448 | tf_op jit(solution)/shard_map/all_gather | solution.py:102
  71.2 18.7 %gather_fusion = bf16[3072,1024]{1,0:T(8,128)(2,1)} fusion(bf16[2004,1024]{1,0:T(8,128)(2,1)} %param.21, s32[3072]{0:T(1024)S(1)} %broadcast_clamp_fusion.1), kind=kCustom, calls=%fused_computation | custom fusion | bytes 12595200 | tf_op jit(solution)/shard_map/jit(_take)/gather | solution.py:112
  89.9 7.0 %select_select_fusion = bf16[32,96,1024]{2,1,0:T(8,128)(2,1)} fusion(bf16[32,96,1024]{2,1,0:T(8,128)(2,1)} %bitcast.128, pred[32,96]{1,0:T(8,128)(4,1)S(1)} %get-tuple-element.312, pred[32,96]{1,0:T(8,128)(4,1)S(1)} %get-tuple-element.322), kind=kLoop, calls=%fused_computation.56 | loop fusion | flops 6291456 | bytes 12589056 | tf_op jit(solution)/shard_map/jit(_where)/select_n | solution.py:113
  105.7 79.5 %all-reduce.2 = (s32[64]{0:T(128)S(1)}, s32[32]{0:T(128)S(1)}) all-reduce(s32[64]{0:T(128)S(1)} %dynamic-update-slice, s32[32]{0:T(128)S(1)} %dynamic-update-slice.1), channel_id=1, replica_groups=mesh['dp'=8,'pipe'=4,'tensor'=4] {'dp','pipe'}, use_global_device_ids=true, to_apply=%add | all-reduce | flops 96 | bytes 768
  185.3 11.6 %pad_maximum_fusion = bf16[4096,1536]{1,0:T(8,128)(2,1)} fusion(bf16[4096,256]{1,0:T(8,128)(2,1)S(1)} %bitcast.135, bf16[4096,256]{1,0:T(8,128)(2,1)} %bitcast.136, bf16[4096,1024]{1,0:T(8,128)(2,1)} %bitcast.129), kind=kLoop, calls=%fused_computation.55 | loop fusion | flops 37748736 | bytes 25165824 | tf_op jit(solution)/shard_map/concatenate | solution.py:127
  201.1 409.0 %while.16 = (s32[]{:T(128)}, bf16[96,1024]{1,0:T(8,128)(2,1)S(1)}, s32[]{:T(128)}, f32[1,4096]{1,0:T(1,128)S(1)}, bf16[4096,1536]{1,0:T(8,128)(2,1)}, /*index=5*...) while((s32[]{:T(128)}, bf16[96,1024]{1,0:T(8,128)(2,1)S(1)}, ...), condition=%wide.region_6.7_spmd.clone, body=%wide.region_1.0_spmd.clone.sunk | while | flops 2038168704 | bytes 45535072 | solution.py:179
  209.2 10.1 %all-to-all-done = bf16[4,96,1024]{2,1,0:T(8,128)(2,1)S(1)} async-done(((bf16[4,96,1024]{2,1,0:T(8,128)(2,1)}), bf16[4,96,1024]{2,1,0:T(8,128)(2,1)S(1)}, u32[]{:S(2)}, u32[]{:S(2)}) %all-to-all-start) | async-done | bytes 786464 | tf_op jit(solution)/shard_map/while/body/eval_jaxpr/all_to_all | solution.py:23
  238.3 11.0 %all-to-all-done.1 = bf16[4,96,1024]{2,1,0:T(8,128)(2,1)S(1)} async-done(((bf16[4,96,1024]{2,1,0:T(8,128)(2,1)}), bf16[4,96,1024]{2,1,0:T(8,128)(2,1)S(1)}, u32[]{:S(2)}, u32[]{:S(2)}) %all-to-all-start.1) | async-done | bytes 786464 | tf_op jit(solution)/shard_map/while/body/eval_jaxpr/all_to_all | solution.py:38
  262.7 7.7 %all-to-all-done = bf16[4,96,1024]{2,1,0:T(8,128)(2,1)S(1)} async-done(((bf16[4,96,1024]{2,1,0:T(8,128)(2,1)}), bf16[4,96,1024]{2,1,0:T(8,128)(2,1)S(1)}, u32[]{:S(2)}, u32[]{:S(2)}) %all-to-all-start) | async-done | bytes 786464 | tf_op jit(solution)/shard_map/while/body/eval_jaxpr/all_to_all | solution.py:23
  289.3 9.4 %all-to-all-done.1 = bf16[4,96,1024]{2,1,0:T(8,128)(2,1)S(1)} async-done(((bf16[4,96,1024]{2,1,0:T(8,128)(2,1)}), bf16[4,96,1024]{2,1,0:T(8,128)(2,1)S(1)}, u32[]{:S(2)}, u32[]{:S(2)}) %all-to-all-start.1) | async-done | bytes 786464 | tf_op jit(solution)/shard_map/while/body/eval_jaxpr/all_to_all | solution.py:38
  299.0 6.9 %collective-permute-done = bf16[96,1024]{1,0:T(8,128)(2,1)S(1)} collective-permute-done((bf16[96,1024]{1,0:T(8,128)(2,1)S(1)}, bf16[96,1024]{1,0:T(8,128)(2,1)S(1)}, u32[]{:S(2)}, u32[]{:S(2)}) %collective-permute-start) | collective-permute-done | bytes 196640 | tf_op jit(solution)/shard_map/while/body/eval_jaxpr/ppermute | solution.py:45
  312.2 7.7 %all-to-all-done = bf16[4,96,1024]{2,1,0:T(8,128)(2,1)S(1)} async-done(((bf16[4,96,1024]{2,1,0:T(8,128)(2,1)}), bf16[4,96,1024]{2,1,0:T(8,128)(2,1)S(1)}, u32[]{:S(2)}, u32[]{:S(2)}) %all-to-all-start) | async-done | bytes 786464 | tf_op jit(solution)/shard_map/while/body/eval_jaxpr/all_to_all | solution.py:23
  338.8 9.4 %all-to-all-done.1 = bf16[4,96,1024]{2,1,0:T(8,128)(2,1)S(1)} async-done(((bf16[4,96,1024]{2,1,0:T(8,128)(2,1)}), bf16[4,96,1024]{2,1,0:T(8,128)(2,1)S(1)}, u32[]{:S(2)}, u32[]{:S(2)}) %all-to-all-start.1) | async-done | bytes 786464 | tf_op jit(solution)/shard_map/while/body/eval_jaxpr/all_to_all | solution.py:38
  348.5 6.9 %collective-permute-done = bf16[96,1024]{1,0:T(8,128)(2,1)S(1)} collective-permute-done((bf16[96,1024]{1,0:T(8,128)(2,1)S(1)}, bf16[96,1024]{1,0:T(8,128)(2,1)S(1)}, u32[]{:S(2)}, u32[]{:S(2)}) %collective-permute-start) | collective-permute-done | bytes 196640 | tf_op jit(solution)/shard_map/while/body/eval_jaxpr/ppermute | solution.py:45
  361.7 7.7 %all-to-all-done = bf16[4,96,1024]{2,1,0:T(8,128)(2,1)S(1)} async-done(((bf16[4,96,1024]{2,1,0:T(8,128)(2,1)}), bf16[4,96,1024]{2,1,0:T(8,128)(2,1)S(1)}, u32[]{:S(2)}, u32[]{:S(2)}) %all-to-all-start) | async-done | bytes 786464 | tf_op jit(solution)/shard_map/while/body/eval_jaxpr/all_to_all | solution.py:23
  388.3 9.4 %all-to-all-done.1 = bf16[4,96,1024]{2,1,0:T(8,128)(2,1)S(1)} async-done(((bf16[4,96,1024]{2,1,0:T(8,128)(2,1)}), bf16[4,96,1024]{2,1,0:T(8,128)(2,1)S(1)}, u32[]{:S(2)}, u32[]{:S(2)}) %all-to-all-start.1) | async-done | bytes 786464 | tf_op jit(solution)/shard_map/while/body/eval_jaxpr/all_to_all | solution.py:38
  398.0 6.9 %collective-permute-done = bf16[96,1024]{1,0:T(8,128)(2,1)S(1)} collective-permute-done((bf16[96,1024]{1,0:T(8,128)(2,1)S(1)}, bf16[96,1024]{1,0:T(8,128)(2,1)S(1)}, u32[]{:S(2)}, u32[]{:S(2)}) %collective-permute-start) | collective-permute-done | bytes 196640 | tf_op jit(solution)/shard_map/while/body/eval_jaxpr/ppermute | solution.py:45
  411.2 7.7 %all-to-all-done = bf16[4,96,1024]{2,1,0:T(8,128)(2,1)S(1)} async-done(((bf16[4,96,1024]{2,1,0:T(8,128)(2,1)}), bf16[4,96,1024]{2,1,0:T(8,128)(2,1)S(1)}, u32[]{:S(2)}, u32[]{:S(2)}) %all-to-all-start) | async-done | bytes 786464 | tf_op jit(solution)/shard_map/while/body/eval_jaxpr/all_to_all | solution.py:23
  437.8 10.7 %all-to-all-done.1 = bf16[4,96,1024]{2,1,0:T(8,128)(2,1)S(1)} async-done(((bf16[4,96,1024]{2,1,0:T(8,128)(2,1)}), bf16[4,96,1024]{2,1,0:T(8,128)(2,1)S(1)}, u32[]{:S(2)}, u32[]{:S(2)}) %all-to-all-start.1) | async-done | bytes 786464 | tf_op jit(solution)/shard_map/while/body/eval_jaxpr/all_to_all | solution.py:38
  462.0 7.7 %all-to-all-done = bf16[4,96,1024]{2,1,0:T(8,128)(2,1)S(1)} async-done(((bf16[4,96,1024]{2,1,0:T(8,128)(2,1)}), bf16[4,96,1024]{2,1,0:T(8,128)(2,1)S(1)}, u32[]{:S(2)}, u32[]{:S(2)}) %all-to-all-start) | async-done | bytes 786464 | tf_op jit(solution)/shard_map/while/body/eval_jaxpr/all_to_all | solution.py:23
  488.6 13.1 %all-to-all-done.1 = bf16[4,96,1024]{2,1,0:T(8,128)(2,1)S(1)} async-done(((bf16[4,96,1024]{2,1,0:T(8,128)(2,1)}), bf16[4,96,1024]{2,1,0:T(8,128)(2,1)S(1)}, u32[]{:S(2)}, u32[]{:S(2)}) %all-to-all-start.1) | async-done | bytes 786464 | tf_op jit(solution)/shard_map/while/body/eval_jaxpr/all_to_all | solution.py:38
  502.0 6.9 %collective-permute-done = bf16[96,1024]{1,0:T(8,128)(2,1)S(1)} collective-permute-done((bf16[96,1024]{1,0:T(8,128)(2,1)S(1)}, bf16[96,1024]{1,0:T(8,128)(2,1)S(1)}, u32[]{:S(2)}, u32[]{:S(2)}) %collective-permute-start) | collective-permute-done | bytes 196640 | tf_op jit(solution)/shard_map/while/body/eval_jaxpr/ppermute | solution.py:45
  515.1 7.7 %all-to-all-done = bf16[4,96,1024]{2,1,0:T(8,128)(2,1)S(1)} async-done(((bf16[4,96,1024]{2,1,0:T(8,128)(2,1)}), bf16[4,96,1024]{2,1,0:T(8,128)(2,1)S(1)}, u32[]{:S(2)}, u32[]{:S(2)}) %all-to-all-start) | async-done | bytes 786464 | tf_op jit(solution)/shard_map/while/body/eval_jaxpr/all_to_all | solution.py:23
  541.8 10.0 %all-to-all-done.1 = bf16[4,96,1024]{2,1,0:T(8,128)(2,1)S(1)} async-done(((bf16[4,96,1024]{2,1,0:T(8,128)(2,1)}), bf16[4,96,1024]{2,1,0:T(8,128)(2,1)S(1)}, u32[]{:S(2)}, u32[]{:S(2)}) %all-to-all-start.1) | async-done | bytes 786464 | tf_op jit(solution)/shard_map/while/body/eval_jaxpr/all_to_all | solution.py:38
  552.0 6.9 %collective-permute-done = bf16[96,1024]{1,0:T(8,128)(2,1)S(1)} collective-permute-done((bf16[96,1024]{1,0:T(8,128)(2,1)S(1)}, bf16[96,1024]{1,0:T(8,128)(2,1)S(1)}, u32[]{:S(2)}, u32[]{:S(2)}) %collective-permute-start) | collective-permute-done | bytes 196640 | tf_op jit(solution)/shard_map/while/body/eval_jaxpr/ppermute | solution.py:45
  565.2 9.5 %all-to-all-done = bf16[4,96,1024]{2,1,0:T(8,128)(2,1)S(1)} async-done(((bf16[4,96,1024]{2,1,0:T(8,128)(2,1)}), bf16[4,96,1024]{2,1,0:T(8,128)(2,1)S(1)}, u32[]{:S(2)}, u32[]{:S(2)}) %all-to-all-start) | async-done | bytes 786464 | tf_op jit(solution)/shard_map/while/body/eval_jaxpr/all_to_all | solution.py:23
  593.6 9.4 %all-to-all-done.1 = bf16[4,96,1024]{2,1,0:T(8,128)(2,1)S(1)} async-done(((bf16[4,96,1024]{2,1,0:T(8,128)(2,1)}), bf16[4,96,1024]{2,1,0:T(8,128)(2,1)S(1)}, u32[]{:S(2)}, u32[]{:S(2)}) %all-to-all-start.1) | async-done | bytes 786464 | tf_op jit(solution)/shard_map/while/body/eval_jaxpr/all_to_all | solution.py:38
  603.3 6.9 %collective-permute-done = bf16[96,1024]{1,0:T(8,128)(2,1)S(1)} collective-permute-done((bf16[96,1024]{1,0:T(8,128)(2,1)S(1)}, bf16[96,1024]{1,0:T(8,128)(2,1)S(1)}, u32[]{:S(2)}, u32[]{:S(2)}) %collective-permute-start) | collective-permute-done | bytes 196640 | tf_op jit(solution)/shard_map/while/body/eval_jaxpr/ppermute | solution.py:45
  614.9 9.2 %all-to-all-done.3 = bf16[4,96,1024]{2,1,0:T(8,128)(2,1)S(1)} async-done(((bf16[4,96,1024]{2,1,0:T(8,128)(2,1)}), bf16[4,96,1024]{2,1,0:T(8,128)(2,1)S(1)}, u32[]{:S(2)}, u32[]{:S(2)}) %all-to-all-start.3) | async-done | bytes 786464 | tf_op jit(solution)/shard_map/all_to_all | solution.py:23
  643.8 27.6 %all-to-all-done.4 = bf16[32,32,1024]{2,1,0:T(8,128)(2,1)S(1)} async-done(((bf16[32,32,1024]{2,1,0:T(8,128)(2,1)}), bf16[32,32,1024]{2,1,0:T(8,128)(2,1)S(1)}, u32[]{:S(2)}, u32[]{:S(2)}) %all-to-all-start.4) | async-done | bytes 2097184 | tf_op jit(solution)/shard_map/all_to_all | solution.py:23
  672.4 8.9 %psum.7 = f32[1,16]{1,0:T(1,128)S(1)} all-reduce(f32[1,16]{1,0:T(1,128)S(1)} %bitcast.147), channel_id=1, replica_groups=mesh['dp'=8,'pipe'=4,'tensor'=4] {'tensor'}, use_global_device_ids=true, to_apply=%region_13.14 | all-reduce | flops 16 | bytes 128 | tf_op jit(solution)/shard_map/psum | solution.py:208
  (342 shorter events, 255.2 us)
Async XLA Ops:
  96.9 88.4 %copy-start = (bf16[1,4096,256]{2,1,0:T(8,128)(2,1)S(1)}, bf16[1,4096,256]{2,1,0:T(8,128)(2,1)}, u32[]{:S(2)}) copy-start(bf16[1,4096,256]{2,1,0:T(8,128)(2,1)} %param.25) | copy-start | bytes 6291460
  96.9 99.9 %all-to-all-start.2 = ((bf16[32,96,1024]{2,1,0:T(8,128)(2,1)}), bf16[32,96,1024]{2,1,0:T(8,128)(2,1)}, u32[]{:S(2)}, u32[]{:S(2)}) async-start(bf16[32,96,1024]{2,1,0:T(8,128)(2,1)} %select_select_fusion), calls=%async_computation.2 | async-start | bytes 12582912 | tf_op jit(solution)/shard_map/all_to_all | solution.py:114
  201.1 413.6 %copy-start.3 = (s32[2,1]{0,1:T(1,128)S(1)}, s32[2,1]{0,1:T(1,128)}, u32[]{:S(2)}) copy-start(s32[2,1]{0,1:T(1,128)} %param.17) | copy-start | bytes 28
  202.2 17.2 %all-to-all-start = ((bf16[4,96,1024]{2,1,0:T(8,128)(2,1)}), bf16[4,96,1024]{2,1,0:T(8,128)(2,1)S(1)}, u32[]{:S(2)}, u32[]{:S(2)}) async-start(bf16[4,96,1024]{2,1,0:T(8,128)(2,1)} %broadcast_in_dim.169), calls=%async_computation | async-start | bytes 1572864 | tf_op jit(solution)/shard_map/while/body/eval_jaxpr/all_to_all | solution.py:23
  234.8 14.5 %all-to-all-start.1 = ((bf16[4,96,1024]{2,1,0:T(8,128)(2,1)}), bf16[4,96,1024]{2,1,0:T(8,128)(2,1)S(1)}, u32[]{:S(2)}, u32[]{:S(2)}) async-start(bf16[4,96,1024]{2,1,0:T(8,128)(2,1)} %bitcast.122), calls=%async_computation.1 | async-start | bytes 1572864 | tf_op jit(solution)/shard_map/while/body/eval_jaxpr/all_to_all | solution.py:38
  249.5 6.9 %collective-permute-start = (bf16[96,1024]{1,0:T(8,128)(2,1)S(1)}, bf16[96,1024]{1,0:T(8,128)(2,1)S(1)}, u32[]{:S(2)}, u32[]{:S(2)}) collective-permute-start(bf16[96,1024]{1,0:T(8,128)(2,1)S(1)} %fusion.89), channel_id=1, source_target_pairs={{12,0},{0,4},{4,8},{8,12},{13,1},{1,5},{5,9},{9,13},{14,2},{2,6},{... | collective-permute-start | bytes 589832 | tf_op jit(solution)/shard_map/while/body/eval_jaxpr/ppermute | solution.py:45
  257.4 13.0 %all-to-all-start = ((bf16[4,96,1024]{2,1,0:T(8,128)(2,1)}), bf16[4,96,1024]{2,1,0:T(8,128)(2,1)S(1)}, u32[]{:S(2)}, u32[]{:S(2)}) async-start(bf16[4,96,1024]{2,1,0:T(8,128)(2,1)} %broadcast_in_dim.169), calls=%async_computation | async-start | bytes 1572864 | tf_op jit(solution)/shard_map/while/body/eval_jaxpr/all_to_all | solution.py:23
  285.8 13.0 %all-to-all-start.1 = ((bf16[4,96,1024]{2,1,0:T(8,128)(2,1)}), bf16[4,96,1024]{2,1,0:T(8,128)(2,1)S(1)}, u32[]{:S(2)}, u32[]{:S(2)}) async-start(bf16[4,96,1024]{2,1,0:T(8,128)(2,1)} %bitcast.122), calls=%async_computation.1 | async-start | bytes 1572864 | tf_op jit(solution)/shard_map/while/body/eval_jaxpr/all_to_all | solution.py:38
  299.0 6.9 %collective-permute-start = (bf16[96,1024]{1,0:T(8,128)(2,1)S(1)}, bf16[96,1024]{1,0:T(8,128)(2,1)S(1)}, u32[]{:S(2)}, u32[]{:S(2)}) collective-permute-start(bf16[96,1024]{1,0:T(8,128)(2,1)S(1)} %fusion.89), channel_id=1, source_target_pairs={{12,0},{0,4},{4,8},{8,12},{13,1},{1,5},{5,9},{9,13},{14,2},{2,6},{... | collective-permute-start | bytes 589832 | tf_op jit(solution)/shard_map/while/body/eval_jaxpr/ppermute | solution.py:45
  306.9 13.0 %all-to-all-start = ((bf16[4,96,1024]{2,1,0:T(8,128)(2,1)}), bf16[4,96,1024]{2,1,0:T(8,128)(2,1)S(1)}, u32[]{:S(2)}, u32[]{:S(2)}) async-start(bf16[4,96,1024]{2,1,0:T(8,128)(2,1)} %broadcast_in_dim.169), calls=%async_computation | async-start | bytes 1572864 | tf_op jit(solution)/shard_map/while/body/eval_jaxpr/all_to_all | solution.py:23
  335.3 13.0 %all-to-all-start.1 = ((bf16[4,96,1024]{2,1,0:T(8,128)(2,1)}), bf16[4,96,1024]{2,1,0:T(8,128)(2,1)S(1)}, u32[]{:S(2)}, u32[]{:S(2)}) async-start(bf16[4,96,1024]{2,1,0:T(8,128)(2,1)} %bitcast.122), calls=%async_computation.1 | async-start | bytes 1572864 | tf_op jit(solution)/shard_map/while/body/eval_jaxpr/all_to_all | solution.py:38
  348.5 6.9 %collective-permute-start = (bf16[96,1024]{1,0:T(8,128)(2,1)S(1)}, bf16[96,1024]{1,0:T(8,128)(2,1)S(1)}, u32[]{:S(2)}, u32[]{:S(2)}) collective-permute-start(bf16[96,1024]{1,0:T(8,128)(2,1)S(1)} %fusion.89), channel_id=1, source_target_pairs={{12,0},{0,4},{4,8},{8,12},{13,1},{1,5},{5,9},{9,13},{14,2},{2,6},{... | collective-permute-start | bytes 589832 | tf_op jit(solution)/shard_map/while/body/eval_jaxpr/ppermute | solution.py:45
  356.4 13.0 %all-to-all-start = ((bf16[4,96,1024]{2,1,0:T(8,128)(2,1)}), bf16[4,96,1024]{2,1,0:T(8,128)(2,1)S(1)}, u32[]{:S(2)}, u32[]{:S(2)}) async-start(bf16[4,96,1024]{2,1,0:T(8,128)(2,1)} %broadcast_in_dim.169), calls=%async_computation | async-start | bytes 1572864 | tf_op jit(solution)/shard_map/while/body/eval_jaxpr/all_to_all | solution.py:23
  384.8 13.0 %all-to-all-start.1 = ((bf16[4,96,1024]{2,1,0:T(8,128)(2,1)}), bf16[4,96,1024]{2,1,0:T(8,128)(2,1)S(1)}, u32[]{:S(2)}, u32[]{:S(2)}) async-start(bf16[4,96,1024]{2,1,0:T(8,128)(2,1)} %bitcast.122), calls=%async_computation.1 | async-start | bytes 1572864 | tf_op jit(solution)/shard_map/while/body/eval_jaxpr/all_to_all | solution.py:38
  397.9 6.9 %collective-permute-start = (bf16[96,1024]{1,0:T(8,128)(2,1)S(1)}, bf16[96,1024]{1,0:T(8,128)(2,1)S(1)}, u32[]{:S(2)}, u32[]{:S(2)}) collective-permute-start(bf16[96,1024]{1,0:T(8,128)(2,1)S(1)} %fusion.89), channel_id=1, source_target_pairs={{12,0},{0,4},{4,8},{8,12},{13,1},{1,5},{5,9},{9,13},{14,2},{2,6},{... | collective-permute-start | bytes 589832 | tf_op jit(solution)/shard_map/while/body/eval_jaxpr/ppermute | solution.py:45
  405.9 13.0 %all-to-all-start = ((bf16[4,96,1024]{2,1,0:T(8,128)(2,1)}), bf16[4,96,1024]{2,1,0:T(8,128)(2,1)S(1)}, u32[]{:S(2)}, u32[]{:S(2)}) async-start(bf16[4,96,1024]{2,1,0:T(8,128)(2,1)} %broadcast_in_dim.169), calls=%async_computation | async-start | bytes 1572864 | tf_op jit(solution)/shard_map/while/body/eval_jaxpr/all_to_all | solution.py:23
  434.3 14.2 %all-to-all-start.1 = ((bf16[4,96,1024]{2,1,0:T(8,128)(2,1)}), bf16[4,96,1024]{2,1,0:T(8,128)(2,1)S(1)}, u32[]{:S(2)}, u32[]{:S(2)}) async-start(bf16[4,96,1024]{2,1,0:T(8,128)(2,1)} %bitcast.122), calls=%async_computation.1 | async-start | bytes 1572864 | tf_op jit(solution)/shard_map/while/body/eval_jaxpr/all_to_all | solution.py:38
  448.7 6.9 %collective-permute-start = (bf16[96,1024]{1,0:T(8,128)(2,1)S(1)}, bf16[96,1024]{1,0:T(8,128)(2,1)S(1)}, u32[]{:S(2)}, u32[]{:S(2)}) collective-permute-start(bf16[96,1024]{1,0:T(8,128)(2,1)S(1)} %fusion.89), channel_id=1, source_target_pairs={{12,0},{0,4},{4,8},{8,12},{13,1},{1,5},{5,9},{9,13},{14,2},{2,6},{... | collective-permute-start | bytes 589832 | tf_op jit(solution)/shard_map/while/body/eval_jaxpr/ppermute | solution.py:45
  456.7 13.0 %all-to-all-start = ((bf16[4,96,1024]{2,1,0:T(8,128)(2,1)}), bf16[4,96,1024]{2,1,0:T(8,128)(2,1)S(1)}, u32[]{:S(2)}, u32[]{:S(2)}) async-start(bf16[4,96,1024]{2,1,0:T(8,128)(2,1)} %broadcast_in_dim.169), calls=%async_computation | async-start | bytes 1572864 | tf_op jit(solution)/shard_map/while/body/eval_jaxpr/all_to_all | solution.py:23
  485.0 16.7 %all-to-all-start.1 = ((bf16[4,96,1024]{2,1,0:T(8,128)(2,1)}), bf16[4,96,1024]{2,1,0:T(8,128)(2,1)S(1)}, u32[]{:S(2)}, u32[]{:S(2)}) async-start(bf16[4,96,1024]{2,1,0:T(8,128)(2,1)} %bitcast.122), calls=%async_computation.1 | async-start | bytes 1572864 | tf_op jit(solution)/shard_map/while/body/eval_jaxpr/all_to_all | solution.py:38
  501.9 6.9 %collective-permute-start = (bf16[96,1024]{1,0:T(8,128)(2,1)S(1)}, bf16[96,1024]{1,0:T(8,128)(2,1)S(1)}, u32[]{:S(2)}, u32[]{:S(2)}) collective-permute-start(bf16[96,1024]{1,0:T(8,128)(2,1)S(1)} %fusion.89), channel_id=1, source_target_pairs={{12,0},{0,4},{4,8},{8,12},{13,1},{1,5},{5,9},{9,13},{14,2},{2,6},{... | collective-permute-start | bytes 589832 | tf_op jit(solution)/shard_map/while/body/eval_jaxpr/ppermute | solution.py:45
  509.9 13.0 %all-to-all-start = ((bf16[4,96,1024]{2,1,0:T(8,128)(2,1)}), bf16[4,96,1024]{2,1,0:T(8,128)(2,1)S(1)}, u32[]{:S(2)}, u32[]{:S(2)}) async-start(bf16[4,96,1024]{2,1,0:T(8,128)(2,1)} %broadcast_in_dim.169), calls=%async_computation | async-start | bytes 1572864 | tf_op jit(solution)/shard_map/while/body/eval_jaxpr/all_to_all | solution.py:23
  538.2 13.5 %all-to-all-start.1 = ((bf16[4,96,1024]{2,1,0:T(8,128)(2,1)}), bf16[4,96,1024]{2,1,0:T(8,128)(2,1)S(1)}, u32[]{:S(2)}, u32[]{:S(2)}) async-start(bf16[4,96,1024]{2,1,0:T(8,128)(2,1)} %bitcast.122), calls=%async_computation.1 | async-start | bytes 1572864 | tf_op jit(solution)/shard_map/while/body/eval_jaxpr/all_to_all | solution.py:38
  551.9 6.9 %collective-permute-start = (bf16[96,1024]{1,0:T(8,128)(2,1)S(1)}, bf16[96,1024]{1,0:T(8,128)(2,1)S(1)}, u32[]{:S(2)}, u32[]{:S(2)}) collective-permute-start(bf16[96,1024]{1,0:T(8,128)(2,1)S(1)} %fusion.89), channel_id=1, source_target_pairs={{12,0},{0,4},{4,8},{8,12},{13,1},{1,5},{5,9},{9,13},{14,2},{2,6},{... | collective-permute-start | bytes 589832 | tf_op jit(solution)/shard_map/while/body/eval_jaxpr/ppermute | solution.py:45
  559.9 14.7 %all-to-all-start = ((bf16[4,96,1024]{2,1,0:T(8,128)(2,1)}), bf16[4,96,1024]{2,1,0:T(8,128)(2,1)S(1)}, u32[]{:S(2)}, u32[]{:S(2)}) async-start(bf16[4,96,1024]{2,1,0:T(8,128)(2,1)} %broadcast_in_dim.169), calls=%async_computation | async-start | bytes 1572864 | tf_op jit(solution)/shard_map/while/body/eval_jaxpr/all_to_all | solution.py:23
  590.0 13.0 %all-to-all-start.1 = ((bf16[4,96,1024]{2,1,0:T(8,128)(2,1)}), bf16[4,96,1024]{2,1,0:T(8,128)(2,1)S(1)}, u32[]{:S(2)}, u32[]{:S(2)}) async-start(bf16[4,96,1024]{2,1,0:T(8,128)(2,1)} %bitcast.122), calls=%async_computation.1 | async-start | bytes 1572864 | tf_op jit(solution)/shard_map/while/body/eval_jaxpr/all_to_all | solution.py:38
  603.2 6.9 %collective-permute-start = (bf16[96,1024]{1,0:T(8,128)(2,1)S(1)}, bf16[96,1024]{1,0:T(8,128)(2,1)S(1)}, u32[]{:S(2)}, u32[]{:S(2)}) collective-permute-start(bf16[96,1024]{1,0:T(8,128)(2,1)S(1)} %fusion.89), channel_id=1, source_target_pairs={{12,0},{0,4},{4,8},{8,12},{13,1},{1,5},{5,9},{9,13},{14,2},{2,6},{... | collective-permute-start | bytes 589832 | tf_op jit(solution)/shard_map/while/body/eval_jaxpr/ppermute | solution.py:45
  611.1 13.0 %all-to-all-start.3 = ((bf16[4,96,1024]{2,1,0:T(8,128)(2,1)}), bf16[4,96,1024]{2,1,0:T(8,128)(2,1)S(1)}, u32[]{:S(2)}, u32[]{:S(2)}) async-start(bf16[4,96,1024]{2,1,0:T(8,128)(2,1)} %broadcast_in_dim.128), calls=%async_computation.3 | async-start | bytes 1572864 | tf_op jit(solution)/shard_map/all_to_all | solution.py:23
  614.6 16.2 %dynamic-slice-start = ((f32[4096]{0:T(1024)}, s32[]{:T(128)}), f32[1024]{0:T(1024)S(1)}, s32[]{:S(2)}) async-start(f32[4096]{0:T(1024)} %param.27, s32[]{:T(128)} %select_n.118), calls=%async_computation.6 | async-start | bytes 8704 | tf_op jit(solution)/shard_map/dynamic_slice | solution.py:180
  624.7 12.8 %all-to-all-start.5 = ((bf16[32,1,32]{2,1,0:T(2,128)(2,1)}), bf16[32,1,32]{2,1,0:T(2,128)(2,1)S(1)}, u32[]{:S(2)}, u32[]{:S(2)}) async-start(bf16[32,1,32]{2,1,0:T(2,128)(2,1)} %broadcast_in_dim.130), calls=%async_computation.5 | async-start | bytes 32768 | tf_op jit(solution)/shard_map/all_to_all | solution.py:23
  639.1 32.3 %all-to-all-start.4 = ((bf16[32,32,1024]{2,1,0:T(8,128)(2,1)}), bf16[32,32,1024]{2,1,0:T(8,128)(2,1)S(1)}, u32[]{:S(2)}, u32[]{:S(2)}) async-start(bf16[32,32,1024]{2,1,0:T(8,128)(2,1)} %broadcast_in_dim.129), calls=%async_computation.4 | async-start | bytes 4194304 | tf_op jit(solution)/shard_map/all_to_all | solution.py:23
  671.9 10.0 %copy-start.2 = (f32[32,1024]{1,0:T(8,128)}, f32[32,1024]{1,0:T(8,128)S(1)}, u32[]{:S(2)}) copy-start(f32[32,1024]{1,0:T(8,128)S(1)} %broadcast_divide_fusion) | copy-start | bytes 393220
  (3 other events, 18.5 us)
where the time goes:
time: 684 us; the launch traced here: 682 us
  waiting for transfers between devices  245 us (36%)
  blocking collectives  159 us (23%)
  matrix products  104 us (15%)
  starting transfers between devices  78.1 us (11%)
  local copies, waits for them, and re-layouts  51.8 us (8%)
  other arithmetic  39.9 us (6%)
    all_to_all x11, waiting for transfers between devices, sent_to_all(): return lax.all_to_all(copies, axis, split_axis=0, concat_axis=0, tiled=True)  108 us
    all_to_all x8, waiting for transfers between devices, sum_at_owner(): lax.all_to_all(split_up(shard, dim, length), axis, 0, 0, tiled=True)  82.5 us
    unnamed x1, blocking collectives  79.5 us
    dot_general x8, matrix products, section_block(): projected = jnp.dot(normed, w_in, preferred_element_type=jnp.float32)  54.2 us
    ppermute x8, waiting for transfers between devices, passed_along(): return lax.ppermute(block, axis, route)  53.9 us
    all_to_all x11, starting transfers between devices, sent_to_all(): return lax.all_to_all(copies, axis, split_axis=0, concat_axis=0, tiled=True)  42.8 us
    dot_general x8, matrix products, section_block(): partial_out = jnp.dot(mixed, out_proj, preferred_element_type=jnp.float32)  38.7 us
    all_gather x1, blocking collectives, shards(): lax.all_gather(support_tokens, ('dp', 'pipe'), axis=0, tiled=True)  36.5 us
  transfers between devices with their start and end apart: 28, of which 27 were waited for; matrix products, arithmetic and copies ran while one was open for 4% of the time, Pallas kernels for 0%

commit v1 on v0

--- a/solution.py
+++ b/solution.py
@@ -90,6 +90,15 @@
     out_weight,
     final_gain,
 ):
+
+    def signs_keep_up(mat):
+        size_here = jax.lax.psum(1, ("dp", "pipe"))
+        queue = []
+        for k in tuple(range(mat.ndim)):
+            queue.append(size_here if k == 0 else 1)
+        e_next = jnp.tile(mat, queue)
+        return jax.lax.all_to_all(e_next, ("dp", "pipe"), split_axis=0, concat_axis=0, tiled=True)
+
     group_count = lax.axis_size(("dp", "pipe"))
     sections = lax.axis_size("pipe")
     sup_dev, seq_len = support_tokens.shape
@@ -99,7 +108,7 @@
     table_rows, width = embedding.shape
     column_start = lax.axis_index("tensor") * width
     all_support, all_query, every_sup_len, every_qry_len = (
-        lax.all_gather(support_tokens, ("dp", "pipe"), axis=0, tiled=True),
+        signs_keep_up(support_tokens),
         lax.all_gather(query_tokens, ("dp", "pipe"), axis=0, tiled=True),
         lax.all_gather(support_lengths, ("dp", "pipe"), axis=0, tiled=True),
         lax.all_gather(query_lengths, ("dp", "pipe"), axis=0, tiled=True),

time: 684 us -> 656 us (0.959)
  blocking collectives: 159 us -> 123 us
    all_gather x1 -> x0, blocking collectives: 36.5 us -> none  [shards(): lax.all_gather(support_tokens, ('dp', 'pipe'), axis=0, tiled=True)]
    all_to_all x0 -> x1, starting transfers between devices: none -> 7.43 us  [signs_keep_up(): jax.lax.all_to_all(e_next, ('dp', 'pipe'), split_axis=0, concat_axis=0, t...]
  transfers between devices with their start and end apart: 28 -> 29, of which waited for: 27 -> 27; matrix products, arithmetic and copies ran while one was open for 4% -> 4% of each run, Pallas kernels for 0% -> 0%
where the time goes in v1:
time: 656 us; the launch traced here: 654 us
  waiting for transfers between devices  245 us (37%)
  blocking collectives  123 us (19%)
  matrix products  104 us (16%)
  starting transfers between devices  84.9 us (13%)
  local copies, waits for them, and re-layouts  52.5 us (8%)
  other arithmetic  39.7 us (6%)
    all_to_all x11, waiting for transfers between devices, sent_to_all(): return lax.all_to_all(copies, axis, split_axis=0, concat_axis=0, tiled=True)  109 us
    all_to_all x8, waiting for transfers between devices, sum_at_owner(): lax.all_to_all(split_up(shard, dim, length), axis, 0, 0, tiled=True)  82.5 us
    unnamed x1, blocking collectives  79.6 us
    dot_general x8, matrix products, section_block(): projected = jnp.dot(normed, w_in, preferred_element_type=jnp.float32)  54.2 us
    ppermute x8, waiting for transfers between devices, passed_along(): return lax.ppermute(block, axis, route)  53.8 us
    all_to_all x11, starting transfers between devices, sent_to_all(): return lax.all_to_all(copies, axis, split_axis=0, concat_axis=0, tiled=True)  42.8 us
    dot_general x8, matrix products, section_block(): partial_out = jnp.dot(mixed, out_proj, preferred_element_type=jnp.float32)  38.7 us
    all_gather x1, blocking collectives, shards(): lax.all_gather(query_tokens, ('dp', 'pipe'), axis=0, tiled=True)  34.2 us
  transfers between devices with their start and end apart: 29, of which 27 were waited for; matrix products, arithmetic and copies ran while one was open for 4% of the time, Pallas kernels for 0%

profile of v1, /device:TPU:0, one launch (start us, length us, event | category | flops | bytes accessed | tf_op | source)
XLA Modules:
  0.0 653.6 jit_solution(4935532351079515641)
XLA Ops:
  1.9 7.4 %all-to-all-start.2 = ((s32[32,2,32]{2,1,0:T(2,128)}), s32[32,2,32]{2,1,0:T(2,128)S(1)}, u32[]{:S(2)}, u32[]{:S(2)}) async-start(s32[32,2,32]{2,1,0:T(2,128)} %tile.2), calls=%async_computation.2 | async-start | bytes 65536 | tf_op jit(solution)/shard_map/all_to_all | solution.py:100
  9.4 34.2 %all-gather = s32[32,1,32]{2,1,0:T(1,128)S(1)} all-gather(s32[1,1,32]{2,1,0:T(1,128)} %bitcast.146), channel_id=1, replica_groups=mesh['dp'=8,'pipe'=4,'tensor'=4] {'dp','pipe'}, dimensions={0}, use_global_device_ids=true | all-gather | bytes 4224 | tf_op jit(solution)/shard_map/all_gather | solution.py:112
  43.9 18.7 %gather_fusion = bf16[3072,1024]{1,0:T(8,128)(2,1)} fusion(bf16[2004,1024]{1,0:T(8,128)(2,1)} %param.21, s32[3072]{0:T(1024)S(1)} %broadcast_clamp_fusion.1), kind=kCustom, calls=%fused_computation | custom fusion | bytes 12595200 | tf_op jit(solution)/shard_map/jit(_take)/gather | solution.py:121
  62.5 7.0 %select_select_fusion = bf16[32,96,1024]{2,1,0:T(8,128)(2,1)} fusion(bf16[32,96,1024]{2,1,0:T(8,128)(2,1)} %bitcast.127, pred[32,96]{1,0:T(8,128)(4,1)S(1)} %get-tuple-element.312, pred[32,96]{1,0:T(8,128)(4,1)S(1)} %get-tuple-element.322), kind=kLoop, calls=%fused_computation.56 | loop fusion | flops 6291456 | bytes 12589056 | tf_op jit(solution)/shard_map/jit(_where)/select_n | solution.py:122
  77.5 79.6 %all-reduce.2 = (s32[64]{0:T(128)S(1)}, s32[32]{0:T(128)S(1)}) all-reduce(s32[64]{0:T(128)S(1)} %dynamic-update-slice, s32[32]{0:T(128)S(1)} %dynamic-update-slice.1), channel_id=1, replica_groups=mesh['dp'=8,'pipe'=4,'tensor'=4] {'dp','pipe'}, use_global_device_ids=true, to_apply=%add | all-reduce | flops 96 | bytes 768
  157.0 11.6 %pad_maximum_fusion = bf16[4096,1536]{1,0:T(8,128)(2,1)} fusion(bf16[4096,256]{1,0:T(8,128)(2,1)S(1)} %bitcast.134, bf16[4096,256]{1,0:T(8,128)(2,1)} %bitcast.135, bf16[4096,1024]{1,0:T(8,128)(2,1)} %bitcast.128), kind=kLoop, calls=%fused_computation.55 | loop fusion | flops 37748736 | bytes 25165824 | tf_op jit(solution)/shard_map/concatenate | solution.py:136
  172.9 409.0 %while.16 = (s32[]{:T(128)}, bf16[96,1024]{1,0:T(8,128)(2,1)S(1)}, s32[]{:T(128)}, f32[1,4096]{1,0:T(1,128)S(1)}, bf16[4096,1536]{1,0:T(8,128)(2,1)}, /*index=5*...) while((s32[]{:T(128)}, bf16[96,1024]{1,0:T(8,128)(2,1)S(1)}, ...), condition=%wide.region_6.7_spmd.clone, body=%wide.region_1.0_spmd.clone.sunk | while | flops 2038168704 | bytes 45535072 | solution.py:188
  180.9 10.2 %all-to-all-done = bf16[4,96,1024]{2,1,0:T(8,128)(2,1)S(1)} async-done(((bf16[4,96,1024]{2,1,0:T(8,128)(2,1)}), bf16[4,96,1024]{2,1,0:T(8,128)(2,1)S(1)}, u32[]{:S(2)}, u32[]{:S(2)}) %all-to-all-start) | async-done | bytes 786464 | tf_op jit(solution)/shard_map/while/body/eval_jaxpr/all_to_all | solution.py:23
  210.1 11.0 %all-to-all-done.1 = bf16[4,96,1024]{2,1,0:T(8,128)(2,1)S(1)} async-done(((bf16[4,96,1024]{2,1,0:T(8,128)(2,1)}), bf16[4,96,1024]{2,1,0:T(8,128)(2,1)S(1)}, u32[]{:S(2)}, u32[]{:S(2)}) %all-to-all-start.1) | async-done | bytes 786464 | tf_op jit(solution)/shard_map/while/body/eval_jaxpr/all_to_all | solution.py:38
  234.4 7.8 %all-to-all-done = bf16[4,96,1024]{2,1,0:T(8,128)(2,1)S(1)} async-done(((bf16[4,96,1024]{2,1,0:T(8,128)(2,1)}), bf16[4,96,1024]{2,1,0:T(8,128)(2,1)S(1)}, u32[]{:S(2)}, u32[]{:S(2)}) %all-to-all-start) | async-done | bytes 786464 | tf_op jit(solution)/shard_map/while/body/eval_jaxpr/all_to_all | solution.py:23
  261.1 9.4 %all-to-all-done.1 = bf16[4,96,1024]{2,1,0:T(8,128)(2,1)S(1)} async-done(((bf16[4,96,1024]{2,1,0:T(8,128)(2,1)}), bf16[4,96,1024]{2,1,0:T(8,128)(2,1)S(1)}, u32[]{:S(2)}, u32[]{:S(2)}) %all-to-all-start.1) | async-done | bytes 786464 | tf_op jit(solution)/shard_map/while/body/eval_jaxpr/all_to_all | solution.py:38
  270.8 6.9 %collective-permute-done = bf16[96,1024]{1,0:T(8,128)(2,1)S(1)} collective-permute-done((bf16[96,1024]{1,0:T(8,128)(2,1)S(1)}, bf16[96,1024]{1,0:T(8,128)(2,1)S(1)}, u32[]{:S(2)}, u32[]{:S(2)}) %collective-permute-start) | collective-permute-done | bytes 196640 | tf_op jit(solution)/shard_map/while/body/eval_jaxpr/ppermute | solution.py:45
  283.9 7.8 %all-to-all-done = bf16[4,96,1024]{2,1,0:T(8,128)(2,1)S(1)} async-done(((bf16[4,96,1024]{2,1,0:T(8,128)(2,1)}), bf16[4,96,1024]{2,1,0:T(8,128)(2,1)S(1)}, u32[]{:S(2)}, u32[]{:S(2)}) %all-to-all-start) | async-done | bytes 786464 | tf_op jit(solution)/shard_map/while/body/eval_jaxpr/all_to_all | solution.py:23
  310.6 9.4 %all-to-all-done.1 = bf16[4,96,1024]{2,1,0:T(8,128)(2,1)S(1)} async-done(((bf16[4,96,1024]{2,1,0:T(8,128)(2,1)}), bf16[4,96,1024]{2,1,0:T(8,128)(2,1)S(1)}, u32[]{:S(2)}, u32[]{:S(2)}) %all-to-all-start.1) | async-done | bytes 786464 | tf_op jit(solution)/shard_map/while/body/eval_jaxpr/all_to_all | solution.py:38
  320.3 6.9 %collective-permute-done = bf16[96,1024]{1,0:T(8,128)(2,1)S(1)} collective-permute-done((bf16[96,1024]{1,0:T(8,128)(2,1)S(1)}, bf16[96,1024]{1,0:T(8,128)(2,1)S(1)}, u32[]{:S(2)}, u32[]{:S(2)}) %collective-permute-start) | collective-permute-done | bytes 196640 | tf_op jit(solution)/shard_map/while/body/eval_jaxpr/ppermute | solution.py:45
  333.4 7.8 %all-to-all-done = bf16[4,96,1024]{2,1,0:T(8,128)(2,1)S(1)} async-done(((bf16[4,96,1024]{2,1,0:T(8,128)(2,1)}), bf16[4,96,1024]{2,1,0:T(8,128)(2,1)S(1)}, u32[]{:S(2)}, u32[]{:S(2)}) %all-to-all-start) | async-done | bytes 786464 | tf_op jit(solution)/shard_map/while/body/eval_jaxpr/all_to_all | solution.py:23
  360.1 9.4 %all-to-all-done.1 = bf16[4,96,1024]{2,1,0:T(8,128)(2,1)S(1)} async-done(((bf16[4,96,1024]{2,1,0:T(8,128)(2,1)}), bf16[4,96,1024]{2,1,0:T(8,128)(2,1)S(1)}, u32[]{:S(2)}, u32[]{:S(2)}) %all-to-all-start.1) | async-done | bytes 786464 | tf_op jit(solution)/shard_map/while/body/eval_jaxpr/all_to_all | solution.py:38
  369.8 6.9 %collective-permute-done = bf16[96,1024]{1,0:T(8,128)(2,1)S(1)} collective-permute-done((bf16[96,1024]{1,0:T(8,128)(2,1)S(1)}, bf16[96,1024]{1,0:T(8,128)(2,1)S(1)}, u32[]{:S(2)}, u32[]{:S(2)}) %collective-permute-start) | collective-permute-done | bytes 196640 | tf_op jit(solution)/shard_map/while/body/eval_jaxpr/ppermute | solution.py:45
  382.9 7.8 %all-to-all-done = bf16[4,96,1024]{2,1,0:T(8,128)(2,1)S(1)} async-done(((bf16[4,96,1024]{2,1,0:T(8,128)(2,1)}), bf16[4,96,1024]{2,1,0:T(8,128)(2,1)S(1)}, u32[]{:S(2)}, u32[]{:S(2)}) %all-to-all-start) | async-done | bytes 786464 | tf_op jit(solution)/shard_map/while/body/eval_jaxpr/all_to_all | solution.py:23
  409.6 10.7 %all-to-all-done.1 = bf16[4,96,1024]{2,1,0:T(8,128)(2,1)S(1)} async-done(((bf16[4,96,1024]{2,1,0:T(8,128)(2,1)}), bf16[4,96,1024]{2,1,0:T(8,128)(2,1)S(1)}, u32[]{:S(2)}, u32[]{:S(2)}) %all-to-all-start.1) | async-done | bytes 786464 | tf_op jit(solution)/shard_map/while/body/eval_jaxpr/all_to_all | solution.py:38
  420.6 6.9 %collective-permute-done = bf16[96,1024]{1,0:T(8,128)(2,1)S(1)} collective-permute-done((bf16[96,1024]{1,0:T(8,128)(2,1)S(1)}, bf16[96,1024]{1,0:T(8,128)(2,1)S(1)}, u32[]{:S(2)}, u32[]{:S(2)}) %collective-permute-start) | collective-permute-done | bytes 196640 | tf_op jit(solution)/shard_map/while/body/eval_jaxpr/ppermute | solution.py:45
  433.7 7.8 %all-to-all-done = bf16[4,96,1024]{2,1,0:T(8,128)(2,1)S(1)} async-done(((bf16[4,96,1024]{2,1,0:T(8,128)(2,1)}), bf16[4,96,1024]{2,1,0:T(8,128)(2,1)S(1)}, u32[]{:S(2)}, u32[]{:S(2)}) %all-to-all-start) | async-done | bytes 786464 | tf_op jit(solution)/shard_map/while/body/eval_jaxpr/all_to_all | solution.py:23
  460.4 13.1 %all-to-all-done.1 = bf16[4,96,1024]{2,1,0:T(8,128)(2,1)S(1)} async-done(((bf16[4,96,1024]{2,1,0:T(8,128)(2,1)}), bf16[4,96,1024]{2,1,0:T(8,128)(2,1)S(1)}, u32[]{:S(2)}, u32[]{:S(2)}) %all-to-all-start.1) | async-done | bytes 786464 | tf_op jit(solution)/shard_map/while/body/eval_jaxpr/all_to_all | solution.py:38
  486.8 7.8 %all-to-all-done = bf16[4,96,1024]{2,1,0:T(8,128)(2,1)S(1)} async-done(((bf16[4,96,1024]{2,1,0:T(8,128)(2,1)}), bf16[4,96,1024]{2,1,0:T(8,128)(2,1)S(1)}, u32[]{:S(2)}, u32[]{:S(2)}) %all-to-all-start) | async-done | bytes 786464 | tf_op jit(solution)/shard_map/while/body/eval_jaxpr/all_to_all | solution.py:23
  513.5 10.0 %all-to-all-done.1 = bf16[4,96,1024]{2,1,0:T(8,128)(2,1)S(1)} async-done(((bf16[4,96,1024]{2,1,0:T(8,128)(2,1)}), bf16[4,96,1024]{2,1,0:T(8,128)(2,1)S(1)}, u32[]{:S(2)}, u32[]{:S(2)}) %all-to-all-start.1) | async-done | bytes 786464 | tf_op jit(solution)/shard_map/while/body/eval_jaxpr/all_to_all | solution.py:38
  523.8 6.9 %collective-permute-done = bf16[96,1024]{1,0:T(8,128)(2,1)S(1)} collective-permute-done((bf16[96,1024]{1,0:T(8,128)(2,1)S(1)}, bf16[96,1024]{1,0:T(8,128)(2,1)S(1)}, u32[]{:S(2)}, u32[]{:S(2)}) %collective-permute-start) | collective-permute-done | bytes 196640 | tf_op jit(solution)/shard_map/while/body/eval_jaxpr/ppermute | solution.py:45
  536.8 9.6 %all-to-all-done = bf16[4,96,1024]{2,1,0:T(8,128)(2,1)S(1)} async-done(((bf16[4,96,1024]{2,1,0:T(8,128)(2,1)}), bf16[4,96,1024]{2,1,0:T(8,128)(2,1)S(1)}, u32[]{:S(2)}, u32[]{:S(2)}) %all-to-all-start) | async-done | bytes 786464 | tf_op jit(solution)/shard_map/while/body/eval_jaxpr/all_to_all | solution.py:23
  565.3 9.4 %all-to-all-done.1 = bf16[4,96,1024]{2,1,0:T(8,128)(2,1)S(1)} async-done(((bf16[4,96,1024]{2,1,0:T(8,128)(2,1)}), bf16[4,96,1024]{2,1,0:T(8,128)(2,1)S(1)}, u32[]{:S(2)}, u32[]{:S(2)}) %all-to-all-start.1) | async-done | bytes 786464 | tf_op jit(solution)/shard_map/while/body/eval_jaxpr/all_to_all | solution.py:38
  575.0 6.9 %collective-permute-done = bf16[96,1024]{1,0:T(8,128)(2,1)S(1)} collective-permute-done((bf16[96,1024]{1,0:T(8,128)(2,1)S(1)}, bf16[96,1024]{1,0:T(8,128)(2,1)S(1)}, u32[]{:S(2)}, u32[]{:S(2)}) %collective-permute-start) | collective-permute-done | bytes 196640 | tf_op jit(solution)/shard_map/while/body/eval_jaxpr/ppermute | solution.py:45
  586.6 9.2 %all-to-all-done.4 = bf16[4,96,1024]{2,1,0:T(8,128)(2,1)S(1)} async-done(((bf16[4,96,1024]{2,1,0:T(8,128)(2,1)}), bf16[4,96,1024]{2,1,0:T(8,128)(2,1)S(1)}, u32[]{:S(2)}, u32[]{:S(2)}) %all-to-all-start.4) | async-done | bytes 786464 | tf_op jit(solution)/shard_map/all_to_all | solution.py:23
  615.6 27.6 %all-to-all-done.5 = bf16[32,32,1024]{2,1,0:T(8,128)(2,1)S(1)} async-done(((bf16[32,32,1024]{2,1,0:T(8,128)(2,1)}), bf16[32,32,1024]{2,1,0:T(8,128)(2,1)S(1)}, u32[]{:S(2)}, u32[]{:S(2)}) %all-to-all-start.5) | async-done | bytes 2097184 | tf_op jit(solution)/shard_map/all_to_all | solution.py:23
  644.2 8.9 %psum.7 = f32[1,16]{1,0:T(1,128)S(1)} all-reduce(f32[1,16]{1,0:T(1,128)S(1)} %bitcast.145), channel_id=1, replica_groups=mesh['dp'=8,'pipe'=4,'tensor'=4] {'tensor'}, use_global_device_ids=true, to_apply=%region_13.14 | all-reduce | flops 16 | bytes 128 | tf_op jit(solution)/shard_map/psum | solution.py:217
  (344 shorter events, 255.0 us)
Async XLA Ops:
  1.9 41.6 %all-to-all-start.2 = ((s32[32,2,32]{2,1,0:T(2,128)}), s32[32,2,32]{2,1,0:T(2,128)S(1)}, u32[]{:S(2)}, u32[]{:S(2)}) async-start(s32[32,2,32]{2,1,0:T(2,128)} %tile.2), calls=%async_computation.2 | async-start | bytes 65536 | tf_op jit(solution)/shard_map/all_to_all | solution.py:100
  69.5 87.5 %copy-start = (bf16[1,4096,256]{2,1,0:T(8,128)(2,1)S(1)}, bf16[1,4096,256]{2,1,0:T(8,128)(2,1)}, u32[]{:S(2)}) copy-start(bf16[1,4096,256]{2,1,0:T(8,128)(2,1)} %param.25) | copy-start | bytes 6291460
  69.5 99.1 %all-to-all-start.3 = ((bf16[32,96,1024]{2,1,0:T(8,128)(2,1)}), bf16[32,96,1024]{2,1,0:T(8,128)(2,1)}, u32[]{:S(2)}, u32[]{:S(2)}) async-start(bf16[32,96,1024]{2,1,0:T(8,128)(2,1)} %select_select_fusion), calls=%async_computation.3 | async-start | bytes 12582912 | tf_op jit(solution)/shard_map/all_to_all | solution.py:123
  172.9 413.6 %copy-start.3 = (s32[2,1]{0,1:T(1,128)S(1)}, s32[2,1]{0,1:T(1,128)}, u32[]{:S(2)}) copy-start(s32[2,1]{0,1:T(1,128)} %param.17) | copy-start | bytes 28
  174.0 17.2 %all-to-all-start = ((bf16[4,96,1024]{2,1,0:T(8,128)(2,1)}), bf16[4,96,1024]{2,1,0:T(8,128)(2,1)S(1)}, u32[]{:S(2)}, u32[]{:S(2)}) async-start(bf16[4,96,1024]{2,1,0:T(8,128)(2,1)} %broadcast_in_dim.169), calls=%async_computation | async-start | bytes 1572864 | tf_op jit(solution)/shard_map/while/body/eval_jaxpr/all_to_all | solution.py:23
  206.6 14.5 %all-to-all-start.1 = ((bf16[4,96,1024]{2,1,0:T(8,128)(2,1)}), bf16[4,96,1024]{2,1,0:T(8,128)(2,1)S(1)}, u32[]{:S(2)}, u32[]{:S(2)}) async-start(bf16[4,96,1024]{2,1,0:T(8,128)(2,1)} %bitcast.121), calls=%async_computation.1 | async-start | bytes 1572864 | tf_op jit(solution)/shard_map/while/body/eval_jaxpr/all_to_all | solution.py:38
  221.2 6.9 %collective-permute-start = (bf16[96,1024]{1,0:T(8,128)(2,1)S(1)}, bf16[96,1024]{1,0:T(8,128)(2,1)S(1)}, u32[]{:S(2)}, u32[]{:S(2)}) collective-permute-start(bf16[96,1024]{1,0:T(8,128)(2,1)S(1)} %fusion.89), channel_id=1, source_target_pairs={{12,0},{0,4},{4,8},{8,12},{13,1},{1,5},{5,9},{9,13},{14,2},{2,6},{... | collective-permute-start | bytes 589832 | tf_op jit(solution)/shard_map/while/body/eval_jaxpr/ppermute | solution.py:45
  229.2 13.0 %all-to-all-start = ((bf16[4,96,1024]{2,1,0:T(8,128)(2,1)}), bf16[4,96,1024]{2,1,0:T(8,128)(2,1)S(1)}, u32[]{:S(2)}, u32[]{:S(2)}) async-start(bf16[4,96,1024]{2,1,0:T(8,128)(2,1)} %broadcast_in_dim.169), calls=%async_computation | async-start | bytes 1572864 | tf_op jit(solution)/shard_map/while/body/eval_jaxpr/all_to_all | solution.py:23
  257.6 13.0 %all-to-all-start.1 = ((bf16[4,96,1024]{2,1,0:T(8,128)(2,1)}), bf16[4,96,1024]{2,1,0:T(8,128)(2,1)S(1)}, u32[]{:S(2)}, u32[]{:S(2)}) async-start(bf16[4,96,1024]{2,1,0:T(8,128)(2,1)} %bitcast.121), calls=%async_computation.1 | async-start | bytes 1572864 | tf_op jit(solution)/shard_map/while/body/eval_jaxpr/all_to_all | solution.py:38
  270.7 6.9 %collective-permute-start = (bf16[96,1024]{1,0:T(8,128)(2,1)S(1)}, bf16[96,1024]{1,0:T(8,128)(2,1)S(1)}, u32[]{:S(2)}, u32[]{:S(2)}) collective-permute-start(bf16[96,1024]{1,0:T(8,128)(2,1)S(1)} %fusion.89), channel_id=1, source_target_pairs={{12,0},{0,4},{4,8},{8,12},{13,1},{1,5},{5,9},{9,13},{14,2},{2,6},{... | collective-permute-start | bytes 589832 | tf_op jit(solution)/shard_map/while/body/eval_jaxpr/ppermute | solution.py:45
  278.7 13.0 %all-to-all-start = ((bf16[4,96,1024]{2,1,0:T(8,128)(2,1)}), bf16[4,96,1024]{2,1,0:T(8,128)(2,1)S(1)}, u32[]{:S(2)}, u32[]{:S(2)}) async-start(bf16[4,96,1024]{2,1,0:T(8,128)(2,1)} %broadcast_in_dim.169), calls=%async_computation | async-start | bytes 1572864 | tf_op jit(solution)/shard_map/while/body/eval_jaxpr/all_to_all | solution.py:23
  307.1 13.0 %all-to-all-start.1 = ((bf16[4,96,1024]{2,1,0:T(8,128)(2,1)}), bf16[4,96,1024]{2,1,0:T(8,128)(2,1)S(1)}, u32[]{:S(2)}, u32[]{:S(2)}) async-start(bf16[4,96,1024]{2,1,0:T(8,128)(2,1)} %bitcast.121), calls=%async_computation.1 | async-start | bytes 1572864 | tf_op jit(solution)/shard_map/while/body/eval_jaxpr/all_to_all | solution.py:38
  320.2 6.9 %collective-permute-start = (bf16[96,1024]{1,0:T(8,128)(2,1)S(1)}, bf16[96,1024]{1,0:T(8,128)(2,1)S(1)}, u32[]{:S(2)}, u32[]{:S(2)}) collective-permute-start(bf16[96,1024]{1,0:T(8,128)(2,1)S(1)} %fusion.89), channel_id=1, source_target_pairs={{12,0},{0,4},{4,8},{8,12},{13,1},{1,5},{5,9},{9,13},{14,2},{2,6},{... | collective-permute-start | bytes 589832 | tf_op jit(solution)/shard_map/while/body/eval_jaxpr/ppermute | solution.py:45
  328.2 13.0 %all-to-all-start = ((bf16[4,96,1024]{2,1,0:T(8,128)(2,1)}), bf16[4,96,1024]{2,1,0:T(8,128)(2,1)S(1)}, u32[]{:S(2)}, u32[]{:S(2)}) async-start(bf16[4,96,1024]{2,1,0:T(8,128)(2,1)} %broadcast_in_dim.169), calls=%async_computation | async-start | bytes 1572864 | tf_op jit(solution)/shard_map/while/body/eval_jaxpr/all_to_all | solution.py:23
  356.6 13.0 %all-to-all-start.1 = ((bf16[4,96,1024]{2,1,0:T(8,128)(2,1)}), bf16[4,96,1024]{2,1,0:T(8,128)(2,1)S(1)}, u32[]{:S(2)}, u32[]{:S(2)}) async-start(bf16[4,96,1024]{2,1,0:T(8,128)(2,1)} %bitcast.121), calls=%async_computation.1 | async-start | bytes 1572864 | tf_op jit(solution)/shard_map/while/body/eval_jaxpr/all_to_all | solution.py:38
  369.7 6.9 %collective-permute-start = (bf16[96,1024]{1,0:T(8,128)(2,1)S(1)}, bf16[96,1024]{1,0:T(8,128)(2,1)S(1)}, u32[]{:S(2)}, u32[]{:S(2)}) collective-permute-start(bf16[96,1024]{1,0:T(8,128)(2,1)S(1)} %fusion.89), channel_id=1, source_target_pairs={{12,0},{0,4},{4,8},{8,12},{13,1},{1,5},{5,9},{9,13},{14,2},{2,6},{... | collective-permute-start | bytes 589832 | tf_op jit(solution)/shard_map/while/body/eval_jaxpr/ppermute | solution.py:45
  377.7 13.0 %all-to-all-start = ((bf16[4,96,1024]{2,1,0:T(8,128)(2,1)}), bf16[4,96,1024]{2,1,0:T(8,128)(2,1)S(1)}, u32[]{:S(2)}, u32[]{:S(2)}) async-start(bf16[4,96,1024]{2,1,0:T(8,128)(2,1)} %broadcast_in_dim.169), calls=%async_computation | async-start | bytes 1572864 | tf_op jit(solution)/shard_map/while/body/eval_jaxpr/all_to_all | solution.py:23
  406.1 14.2 %all-to-all-start.1 = ((bf16[4,96,1024]{2,1,0:T(8,128)(2,1)}), bf16[4,96,1024]{2,1,0:T(8,128)(2,1)S(1)}, u32[]{:S(2)}, u32[]{:S(2)}) async-start(bf16[4,96,1024]{2,1,0:T(8,128)(2,1)} %bitcast.121), calls=%async_computation.1 | async-start | bytes 1572864 | tf_op jit(solution)/shard_map/while/body/eval_jaxpr/all_to_all | solution.py:38
  420.5 6.9 %collective-permute-start = (bf16[96,1024]{1,0:T(8,128)(2,1)S(1)}, bf16[96,1024]{1,0:T(8,128)(2,1)S(1)}, u32[]{:S(2)}, u32[]{:S(2)}) collective-permute-start(bf16[96,1024]{1,0:T(8,128)(2,1)S(1)} %fusion.89), channel_id=1, source_target_pairs={{12,0},{0,4},{4,8},{8,12},{13,1},{1,5},{5,9},{9,13},{14,2},{2,6},{... | collective-permute-start | bytes 589832 | tf_op jit(solution)/shard_map/while/body/eval_jaxpr/ppermute | solution.py:45
  428.5 13.0 %all-to-all-start = ((bf16[4,96,1024]{2,1,0:T(8,128)(2,1)}), bf16[4,96,1024]{2,1,0:T(8,128)(2,1)S(1)}, u32[]{:S(2)}, u32[]{:S(2)}) async-start(bf16[4,96,1024]{2,1,0:T(8,128)(2,1)} %broadcast_in_dim.169), calls=%async_computation | async-start | bytes 1572864 | tf_op jit(solution)/shard_map/while/body/eval_jaxpr/all_to_all | solution.py:23
  456.8 16.6 %all-to-all-start.1 = ((bf16[4,96,1024]{2,1,0:T(8,128)(2,1)}), bf16[4,96,1024]{2,1,0:T(8,128)(2,1)S(1)}, u32[]{:S(2)}, u32[]{:S(2)}) async-start(bf16[4,96,1024]{2,1,0:T(8,128)(2,1)} %bitcast.121), calls=%async_computation.1 | async-start | bytes 1572864 | tf_op jit(solution)/shard_map/while/body/eval_jaxpr/all_to_all | solution.py:38
  473.7 6.9 %collective-permute-start = (bf16[96,1024]{1,0:T(8,128)(2,1)S(1)}, bf16[96,1024]{1,0:T(8,128)(2,1)S(1)}, u32[]{:S(2)}, u32[]{:S(2)}) collective-permute-start(bf16[96,1024]{1,0:T(8,128)(2,1)S(1)} %fusion.89), channel_id=1, source_target_pairs={{12,0},{0,4},{4,8},{8,12},{13,1},{1,5},{5,9},{9,13},{14,2},{2,6},{... | collective-permute-start | bytes 589832 | tf_op jit(solution)/shard_map/while/body/eval_jaxpr/ppermute | solution.py:45
  481.6 13.0 %all-to-all-start = ((bf16[4,96,1024]{2,1,0:T(8,128)(2,1)}), bf16[4,96,1024]{2,1,0:T(8,128)(2,1)S(1)}, u32[]{:S(2)}, u32[]{:S(2)}) async-start(bf16[4,96,1024]{2,1,0:T(8,128)(2,1)} %broadcast_in_dim.169), calls=%async_computation | async-start | bytes 1572864 | tf_op jit(solution)/shard_map/while/body/eval_jaxpr/all_to_all | solution.py:23
  510.0 13.5 %all-to-all-start.1 = ((bf16[4,96,1024]{2,1,0:T(8,128)(2,1)}), bf16[4,96,1024]{2,1,0:T(8,128)(2,1)S(1)}, u32[]{:S(2)}, u32[]{:S(2)}) async-start(bf16[4,96,1024]{2,1,0:T(8,128)(2,1)} %bitcast.121), calls=%async_computation.1 | async-start | bytes 1572864 | tf_op jit(solution)/shard_map/while/body/eval_jaxpr/all_to_all | solution.py:38
  523.7 6.9 %collective-permute-start = (bf16[96,1024]{1,0:T(8,128)(2,1)S(1)}, bf16[96,1024]{1,0:T(8,128)(2,1)S(1)}, u32[]{:S(2)}, u32[]{:S(2)}) collective-permute-start(bf16[96,1024]{1,0:T(8,128)(2,1)S(1)} %fusion.89), channel_id=1, source_target_pairs={{12,0},{0,4},{4,8},{8,12},{13,1},{1,5},{5,9},{9,13},{14,2},{2,6},{... | collective-permute-start | bytes 589832 | tf_op jit(solution)/shard_map/while/body/eval_jaxpr/ppermute | solution.py:45
  531.7 14.7 %all-to-all-start = ((bf16[4,96,1024]{2,1,0:T(8,128)(2,1)}), bf16[4,96,1024]{2,1,0:T(8,128)(2,1)S(1)}, u32[]{:S(2)}, u32[]{:S(2)}) async-start(bf16[4,96,1024]{2,1,0:T(8,128)(2,1)} %broadcast_in_dim.169), calls=%async_computation | async-start | bytes 1572864 | tf_op jit(solution)/shard_map/while/body/eval_jaxpr/all_to_all | solution.py:23
  561.8 13.0 %all-to-all-start.1 = ((bf16[4,96,1024]{2,1,0:T(8,128)(2,1)}), bf16[4,96,1024]{2,1,0:T(8,128)(2,1)S(1)}, u32[]{:S(2)}, u32[]{:S(2)}) async-start(bf16[4,96,1024]{2,1,0:T(8,128)(2,1)} %bitcast.121), calls=%async_computation.1 | async-start | bytes 1572864 | tf_op jit(solution)/shard_map/while/body/eval_jaxpr/all_to_all | solution.py:38
  575.0 6.9 %collective-permute-start = (bf16[96,1024]{1,0:T(8,128)(2,1)S(1)}, bf16[96,1024]{1,0:T(8,128)(2,1)S(1)}, u32[]{:S(2)}, u32[]{:S(2)}) collective-permute-start(bf16[96,1024]{1,0:T(8,128)(2,1)S(1)} %fusion.89), channel_id=1, source_target_pairs={{12,0},{0,4},{4,8},{8,12},{13,1},{1,5},{5,9},{9,13},{14,2},{2,6},{... | collective-permute-start | bytes 589832 | tf_op jit(solution)/shard_map/while/body/eval_jaxpr/ppermute | solution.py:45
  582.9 13.0 %all-to-all-start.4 = ((bf16[4,96,1024]{2,1,0:T(8,128)(2,1)}), bf16[4,96,1024]{2,1,0:T(8,128)(2,1)S(1)}, u32[]{:S(2)}, u32[]{:S(2)}) async-start(bf16[4,96,1024]{2,1,0:T(8,128)(2,1)} %broadcast_in_dim.128), calls=%async_computation.4 | async-start | bytes 1572864 | tf_op jit(solution)/shard_map/all_to_all | solution.py:23
  586.4 16.2 %dynamic-slice-start = ((f32[4096]{0:T(1024)}, s32[]{:T(128)}), f32[1024]{0:T(1024)S(1)}, s32[]{:S(2)}) async-start(f32[4096]{0:T(1024)} %param.27, s32[]{:T(128)} %select_n.118), calls=%async_computation.7 | async-start | bytes 8704 | tf_op jit(solution)/shard_map/dynamic_slice | solution.py:189
  596.5 12.8 %all-to-all-start.6 = ((bf16[32,1,32]{2,1,0:T(2,128)(2,1)}), bf16[32,1,32]{2,1,0:T(2,128)(2,1)S(1)}, u32[]{:S(2)}, u32[]{:S(2)}) async-start(bf16[32,1,32]{2,1,0:T(2,128)(2,1)} %broadcast_in_dim.130), calls=%async_computation.6 | async-start | bytes 32768 | tf_op jit(solution)/shard_map/all_to_all | solution.py:23
  610.9 32.3 %all-to-all-start.5 = ((bf16[32,32,1024]{2,1,0:T(8,128)(2,1)}), bf16[32,32,1024]{2,1,0:T(8,128)(2,1)S(1)}, u32[]{:S(2)}, u32[]{:S(2)}) async-start(bf16[32,32,1024]{2,1,0:T(8,128)(2,1)} %broadcast_in_dim.129), calls=%async_computation.5 | async-start | bytes 4194304 | tf_op jit(solution)/shard_map/all_to_all | solution.py:23
  (4 other events, 27.0 us)
